TPU v7x, 32 devices: a whole 2x2x4 slice. The times are simulated.
32 devices in a mesh: prow: 2 (over x), pcol: 16 (over z, y, core).
Axes of the slice: x: 2, y: 2, z: 4, core: 2. Of those that a mesh axis runs over, the one named last changes fastest.
Arguments:
- vectors: float32 [32768, 2048], P('prow', 'pcol'), may hold values from -6 to 6
- reflectors: bfloat16 [4, 256, 32768], P(None, 'pcol', 'prow'), may hold values from -0.03125 to 0.03125
- tau_diag: float32 [4, 256], replicated, may hold values from 0.5 to 1.5
- coupling: float32 [4, 256, 256], replicated, may hold values from -0.375 to 0.375
Outputs:
- result: float32 [32768, 2048], P('prow', 'pcol')
All inputs are finite; a program needn't handle non-finite values.
Results may differ from a plain program's by a relative error of at most 0.0003.
Values may be sent and summed in bfloat16 or wider, within the bound.
A program may use at most 128 MiB of HBM per device.

v0:
```python
import jax
import jax.numpy as jnp
from jax import lax
from jax.sharding import PartitionSpec as P


def on_device(vectors, reflectors, tau_diag, coupling):
    count = reflectors.shape[0]
    gathered = lax.all_gather(reflectors, "pcol", axis=1, tiled=True)
    current = vectors
    for position in range(count - 1, -1, -1):
        rows_panel = gathered[position]
        widened = rows_panel.astype(jnp.float32)
        tri_factor = jnp.diag(tau_diag[position]) + jnp.triu(coupling[position], 1)
        partial_sum = jnp.dot(
            widened, current, precision=lax.Precision.HIGHEST, preferred_element_type=jnp.float32
        )
        totals = lax.psum(partial_sum, "prow")
        updates = jnp.dot(
            tri_factor, totals, precision=lax.Precision.HIGHEST, preferred_element_type=jnp.float32
        )
        current = current - lax.dot_general(
            widened,
            updates,
            (((0,), (0,)), ((), ())),
            precision=lax.Precision.HIGHEST,
            preferred_element_type=jnp.float32,
        )
    return current


def solution(mesh):
    return jax.shard_map(
        on_device,
        mesh=mesh,
        in_specs=(P("prow", "pcol"), P(None, "pcol", "prow"), P(), P()),
        out_specs=P("prow", "pcol"),
        check_vma=False,
    )
```

profile of v0, /device:TPU:0, one launch (start us, length us, event | category | flops | bytes accessed | tf_op | source)
XLA Modules:
  0.0 387.4 jit_solution(3231491931866824591)
XLA Ops:
  6.5 0.0 all-gather.2.cloned.1.call-start
  6.5 0.7 all-gather.2.cloned.1.call-update
  7.3 0.0 all-reduce.5.cloned.1.call-start
  7.3 9.0 %copy.5 = f32[16384,128]{0,1:T(8,128)} copy(f32[16384,128]{1,0:T(8,128)} %param.4) | data formatting | bytes 16777216 | tf_op args[0]
  16.3 0.0 copy-start.3
  16.3 0.0 copy-start.4
  16.3 163.4 %all-gather.2.cloned.1.call-done = bf16[4,256,16384]{2,1,0:T(8,128)(2,1)} async-done(((bf16[4,16,16384]{2,1,0:T(8,128)(2,1)}), bf16[4,256,16384]{2,1,0:T(8,128)(2,1)}) %all-gather.2.cloned.1.call-update) | async-done | bytes 33554448 | tf_op jit(solution)/shard_map/all_gather | solution.py:9
  179.7 11.2 %fusion.4 = f32[256,128]{1,0:T(8,128)} fusion(f32[16384,128]{1,0:T(8,128)} %param.4, bf16[4,256,16384]{2,1,0:T(8,128)(2,1)} %all-gather.2.cloned.1.call-done), kind=kOutput, calls=%fused_computation.12 | convolution fusion | flops 6442450944 | bytes 16908288 | tf_op jit(solution)/shard_map/dot_general | solution.py:15
  190.9 0.0 all-reduce.5.cloned.1.call-update
  190.9 0.6 all-reduce.7.cloned.1.call-start
  191.5 0.0 copy-done.3
  191.5 21.1 %all-reduce.5.cloned.1.call-done = f32[256,128]{1,0:T(8,128)} async-done(((f32[256,128]{1,0:T(8,128)}), f32[256,128]{1,0:T(8,128)}) %all-reduce.5.cloned.1.call-update) | async-done | bytes 131088 | tf_op jit(solution)/shard_map/psum | solution.py:18
  212.6 0.0 copy-done.4
  212.6 1.3 fusion.21
  213.9 9.4 %fusion.3 = f32[16384,128]{0,1:T(8,128)S(1)} fusion(f32[16384,128]{0,1:T(8,128)} %copy.5, f32[256,128]{1,0:T(8,128)S(1)} %fusion.21, bf16[4,256,16384]{2,1,0:T(8,128)(2,1)} %all-gather.2.cloned.1.call-done), kind=kOutput, calls=%fused_computation.7 | convolution fusion | flops 6444548096 | bytes 25296896 | tf_op jit(solution)/shard_map/dot_general | solution.py:22
  223.3 0.0 copy-start
  223.3 3.4 copy-done
  226.7 12.5 %fusion.10 = f32[256,128]{0,1:T(8,128)} fusion(f32[16384,128]{0,1:T(8,128)S(1)} %fusion.3, bf16[4,256,16384]{2,1,0:T(8,128)(2,1)} %all-gather.2.cloned.1.call-done), kind=kOutput, calls=%fused_computation.18 | convolution fusion | flops 6442450944 | bytes 16908288 | tf_op jit(solution)/shard_map/dot_general | solution.py:15
  239.2 0.0 all-reduce.7.cloned.1.call-update
  239.2 0.2 all-reduce.9.cloned.1.call-start
  239.4 21.5 %all-reduce.7.cloned.1.call-done = f32[256,128]{0,1:T(8,128)} async-done(((f32[256,128]{0,1:T(8,128)}), f32[256,128]{0,1:T(8,128)}) %all-reduce.7.cloned.1.call-update) | async-done | bytes 131088 | tf_op jit(solution)/shard_map/psum | solution.py:18
  260.9 1.3 fusion.18
  262.2 9.4 %fusion.2 = f32[16384,128]{0,1:T(8,128)S(1)} fusion(f32[16384,128]{0,1:T(8,128)} %copy-done, f32[256,128]{1,0:T(8,128)S(1)} %fusion.18, bf16[4,256,16384]{2,1,0:T(8,128)(2,1)} %all-gather.2.cloned.1.call-done), kind=kOutput, calls=%fused_computation.5 | convolution fusion | flops 6444548096 | bytes 25296896 | tf_op jit(solution)/shard_map/dot_general | solution.py:22
  271.6 0.0 copy-start.1
  271.6 3.4 copy-done.1
  275.0 12.5 %fusion.9 = f32[256,128]{0,1:T(8,128)} fusion(f32[16384,128]{0,1:T(8,128)S(1)} %fusion.2, bf16[4,256,16384]{2,1,0:T(8,128)(2,1)} %all-gather.2.cloned.1.call-done), kind=kOutput, calls=%fused_computation.17 | convolution fusion | flops 6442450944 | bytes 16908288 | tf_op jit(solution)/shard_map/dot_general | solution.py:15
  287.5 0.0 all-reduce.9.cloned.1.call-update
  287.5 0.3 all-reduce.11.cloned.1.call-start
  287.8 21.4 %all-reduce.9.cloned.1.call-done = f32[256,128]{0,1:T(8,128)} async-done(((f32[256,128]{0,1:T(8,128)}), f32[256,128]{0,1:T(8,128)}) %all-reduce.9.cloned.1.call-update) | async-done | bytes 131088 | tf_op jit(solution)/shard_map/psum | solution.py:18
  309.2 1.3 fusion.15
  310.5 9.4 %fusion.1 = f32[16384,128]{0,1:T(8,128)S(1)} fusion(f32[16384,128]{0,1:T(8,128)} %copy-done.1, f32[256,128]{1,0:T(8,128)S(1)} %fusion.15, bf16[4,256,16384]{2,1,0:T(8,128)(2,1)} %all-gather.2.cloned.1.call-done), kind=kOutput, calls=%fused_computation.3 | convolution fusion | flops 6444548096 | bytes 25296896 | tf_op jit(solution)/shard_map/dot_general | solution.py:22
  319.9 0.0 copy-start.2
  319.9 3.4 copy-done.2
  323.3 12.5 %fusion.8 = f32[256,128]{0,1:T(8,128)} fusion(f32[16384,128]{0,1:T(8,128)S(1)} %fusion.1, bf16[4,256,16384]{2,1,0:T(8,128)(2,1)} %all-gather.2.cloned.1.call-done), kind=kOutput, calls=%fused_computation.16 | convolution fusion | flops 6442450944 | bytes 16908288 | tf_op jit(solution)/shard_map/dot_general | solution.py:15
  335.7 0.0 all-reduce.11.cloned.1.call-update
  335.8 21.7 %all-reduce.11.cloned.1.call-done = f32[256,128]{0,1:T(8,128)} async-done(((f32[256,128]{0,1:T(8,128)}), f32[256,128]{0,1:T(8,128)}) %all-reduce.11.cloned.1.call-update) | async-done | bytes 131088 | tf_op jit(solution)/shard_map/psum | solution.py:18
  357.5 1.3 fusion.12
  358.8 12.8 %fusion = f32[16384,128]{0,1:T(8,128)} fusion(f32[16384,128]{0,1:T(8,128)} %copy-done.2, f32[256,128]{1,0:T(8,128)S(1)} %fusion.12, bf16[4,256,16384]{2,1,0:T(8,128)(2,1)} %all-gather.2.cloned.1.call-done), kind=kOutput, calls=%fused_computation.1 | convolution fusion | flops 6444548096 | bytes 25296896 | tf_op jit(solution)/shard_map/dot_general | solution.py:22
  371.6 9.0 %copy.6 = f32[16384,128]{1,0:T(8,128)} copy(f32[16384,128]{0,1:T(8,128)} %fusion) | data formatting | bytes 16777216 | tf_op jit(solution)/shard_map/sub | solution.py:22
  (1 shorter events, 0.0 us)
Async XLA Ops:
  6.5 173.1 %all-gather.2.cloned.1.call-start = ((), (), s32[]{:S(2)}) async-start(), calls=%async_computation | async-start | bytes 35651584 | tf_op jit(solution)/shard_map/all_gather | solution.py:9
  7.3 205.4 %all-reduce.5.cloned.1.call-start = ((), (), s32[]{:S(2)}) async-start(), calls=%async_computation.1 | async-start | bytes 262144 | tf_op jit(solution)/shard_map/psum | solution.py:18
  16.3 175.2 %copy-start.3 = (f32[4,256]{1,0:T(4,128)S(1)}, f32[4,256]{1,0:T(4,128)}, u32[]{:S(2)}) copy-start(f32[4,256]{1,0:T(4,128)} %param.6) | copy-start | bytes 12292
  16.3 196.3 %copy-start.4 = (f32[4,256,256]{2,1,0:T(8,128)S(1)}, f32[4,256,256]{2,1,0:T(8,128)}, u32[]{:S(2)}) copy-start(f32[4,256,256]{2,1,0:T(8,128)} %param.7) | copy-start | bytes 3145732
  190.9 70.0 %all-reduce.7.cloned.1.call-start = ((), (), s32[]{:S(2)}) async-start(), calls=%async_computation.2 | async-start | bytes 262144 | tf_op jit(solution)/shard_map/psum | solution.py:18
  223.3 3.4 copy-start
  239.2 70.0 %all-reduce.9.cloned.1.call-start = ((), (), s32[]{:S(2)}) async-start(), calls=%async_computation.3 | async-start | bytes 262144 | tf_op jit(solution)/shard_map/psum | solution.py:18
  271.6 3.4 copy-start.1
  287.5 70.0 %all-reduce.11.cloned.1.call-start = ((), (), s32[]{:S(2)}) async-start(), calls=%async_computation.4 | async-start | bytes 262144 | tf_op jit(solution)/shard_map/psum | solution.py:18
  319.9 3.4 copy-start.2
Sparse Core Ops, SparseCore 0:
  8.9 170.7 all-gather.1
  191.1 21.5 all-reduce.4
  239.3 21.5 all-reduce.6
  287.6 21.5 all-reduce.8
  335.9 21.5 all-reduce.10
where the time goes:
time: 391 us; the launch traced here: 387 us
  waiting for transfers between devices  250 us (64%)
  matrix products  94.8 us (24%)
  local copies, waits for them, and re-layouts  28.2 us (7%)
  between operations  13.5 us (3%)
    all_gather x1, waiting for transfers between devices, on_device(): gathered = lax.all_gather(reflectors, 'pcol', axis=1, tiled=True)  163 us
    psum x4, waiting for transfers between devices, on_device(): totals = lax.psum(partial_sum, 'prow')  85.7 us
    dot_general x4, matrix products, on_device(): jnp.dot(widened, current, precision=lax.Precision.HIGHEST, preferred_elem...  48.7 us
    dot_general x4, matrix products, on_device(): lax.dot_general(widened, updates, (((0,), (0,)), ((), ())), precision=lax...  40.9 us
    unnamed x11, local copies, waits for them, and re-layouts  19.2 us
    sub x1, local copies, waits for them, and re-layouts, on_device(): current - lax.dot_general(widened, updates, (((0,), (0,)), ((), ())), pre...  8.98 us
  transfers between devices with their start and end apart: 5, of which 5 were waited for; matrix products, arithmetic and copies ran while one was open for 2% of the time, Pallas kernels for 0%

commit v1 on v0

--- a/solution.py
+++ b/solution.py
@@ -6,7 +6,7 @@
 
 def on_device(vectors, reflectors, tau_diag, coupling):
     count = reflectors.shape[0]
-    gathered = lax.all_gather(reflectors, "pcol", axis=1, tiled=True)
+    gathered = jnp.concatenate(lax.all_gather(reflectors, "pcol"), axis=1)
     current = vectors
     for position in range(count - 1, -1, -1):
         rows_panel = gathered[position]

time: 391 us -> 406 us (1.038)
  local copies, waits for them, and re-layouts: 28.2 us -> 51.6 us
  matrix products: 94.8 us -> 90 us
    slice x0 -> x1, local copies, waits for them, and re-layouts: none -> 20.2 us  [on_device(): rows_panel = gathered[position]]
    dot_general x4, matrix products: 48.7 us -> 44.2 us  [on_device(): jnp.dot(widened, current, precision=lax.Precision.HIGHEST, preferred_elem...]
    unnamed x11 -> x13, local copies, waits for them, and re-layouts: 19.2 us -> 22.4 us
where the time goes in v1:
time: 406 us
  waiting for transfers between devices  250 us (62%)
  matrix products  90 us (22%)
  local copies, waits for them, and re-layouts  51.6 us (13%)
  between operations  13.2 us (3%)
    all_gather x1, waiting for transfers between devices, on_device(): gathered = jnp.concatenate(lax.all_gather(reflectors, 'pcol'), axis=1)  163 us
    psum x4, waiting for transfers between devices, on_device(): totals = lax.psum(partial_sum, 'prow')  86.1 us
    dot_general x4, matrix products, on_device(): jnp.dot(widened, current, precision=lax.Precision.HIGHEST, preferred_elem...  44.2 us
    dot_general x4, matrix products, on_device(): lax.dot_general(widened, updates, (((0,), (0,)), ((), ())), precision=lax...  40.6 us
    unnamed x13, local copies, waits for them, and re-layouts  22.4 us
    slice x1, local copies, waits for them, and re-layouts, on_device(): rows_panel = gathered[position]  20.2 us
    sub x1, local copies, waits for them, and re-layouts, on_device(): current - lax.dot_general(widened, updates, (((0,), (0,)), ((), ())), pre...  8.98 us
  transfers between devices with their start and end apart: 5, of which 5 were waited for; matrix products, arithmetic and copies ran while one was open for 2% of the time, Pallas kernels for 0%

profile of v1, /device:TPU:0, one launch (start us, length us, event | category | flops | bytes accessed | tf_op | source)
XLA Modules:
  0.0 405.8 jit_solution(14707609642674171556)
XLA Ops:
  6.5 0.0 all-gather.3.cloned.1.call-start
  6.5 0.7 all-gather.3.cloned.1.call-update
  7.3 0.0 all-reduce.5.cloned.1.call-start
  7.3 9.0 %copy.7 = f32[16384,128]{0,1:T(8,128)} copy(f32[16384,128]{1,0:T(8,128)} %param.4) | data formatting | bytes 16777216 | tf_op args[0]
  16.3 163.4 %all-gather.3.cloned.1.call-done = bf16[64,16,16384]{2,1,0:T(8,128)(2,1)} async-done(((bf16[4,16,16384]{2,1,0:T(8,128)(2,1)}), bf16[64,16,16384]{2,1,0:T(8,128)(2,1)}) %all-gather.3.cloned.1.call-update) | async-done | bytes 33554448 | tf_op jit(solution)/shard_map/all_gather | solution.py:9
  179.7 20.2 %fusion.36 = (bf16[1,16,16,16384]{3,2,0,1:T(8,128)(2,1)}, bf16[1,16,16,16384]{3,2,0,1:T(8,128)(2,1)}, bf16[1,16,16,16384]{3,2,0,1:T(8,128)(2,1)}, bf16[1,16,16,16384]{3,2,0,1:T(8,128)(2,1)S(1)}) fusion(bf16[4,16,16,16384]{3,2,0,1:T(8,128)(2,1)} %bitcast.81), kind=kLoop, calls=%fused_computation.45 | loop fusion | bytes 67108864 | tf_op jit(solution)/shard_map/slice | solution.py:12
  200.0 0.0 copy-start.3
  200.0 3.2 copy-done.3
  203.2 0.0 copy-start.4
  203.2 0.0 copy-start.5
  203.2 10.1 %fusion.38 = f32[256,128]{1,0:T(8,128)} fusion(bf16[256,16384]{1,0:T(8,128)(2,1)S(1)} %bitcast.79, f32[16384,128]{1,0:T(8,128)} %param.4), kind=kOutput, calls=%fused_computation.47 | convolution fusion | flops 6442450944 | bytes 16908288 | tf_op jit(solution)/shard_map/dot_general | solution.py:15
  213.3 0.0 all-reduce.5.cloned.1.call-update
  213.3 0.0 all-reduce.7.cloned.1.call-start
  213.4 0.0 copy-done.4
  213.4 21.6 %all-reduce.5.cloned.1.call-done = f32[256,128]{1,0:T(8,128)} async-done(((f32[256,128]{1,0:T(8,128)}), f32[256,128]{1,0:T(8,128)}) %all-reduce.5.cloned.1.call-update) | async-done | bytes 131088 | tf_op jit(solution)/shard_map/psum | solution.py:18
  235.0 0.0 copy-done.5
  235.0 1.3 fusion.14
  236.3 9.4 %fusion.3 = f32[16384,128]{0,1:T(8,128)S(1)} fusion(f32[16384,128]{0,1:T(8,128)} %copy.7, f32[256,128]{1,0:T(8,128)S(1)} %fusion.14, bf16[256,16384]{1,0:T(8,128)(2,1)} %bitcast.80), kind=kOutput, calls=%fused_computation.7 | convolution fusion | flops 6444548096 | bytes 25296896 | tf_op jit(solution)/shard_map/dot_general | solution.py:22
  245.7 0.0 copy-start
  245.7 3.4 copy-done
  249.1 11.3 %convolution_bitcast_fusion.6 = f32[256,128]{0,1:T(8,128)} fusion(f32[16384,128]{0,1:T(8,128)S(1)} %fusion.3, bf16[256,16384]{1,0:T(8,128)(2,1)} %bitcast.77), kind=kOutput, calls=%fused_computation.10 | convolution fusion | flops 6442450944 | bytes 16908288 | tf_op jit(solution)/shard_map/dot_general | solution.py:15
  260.4 0.0 all-reduce.7.cloned.1.call-update
  260.5 0.2 all-reduce.9.cloned.1.call-start
  260.7 21.4 %all-reduce.7.cloned.1.call-done = f32[256,128]{0,1:T(8,128)} async-done(((f32[256,128]{0,1:T(8,128)}), f32[256,128]{0,1:T(8,128)}) %all-reduce.7.cloned.1.call-update) | async-done | bytes 131088 | tf_op jit(solution)/shard_map/psum | solution.py:18
  282.1 1.3 fusion.11
  283.5 9.4 %fusion.2 = f32[16384,128]{0,1:T(8,128)S(1)} fusion(f32[16384,128]{0,1:T(8,128)} %copy-done, f32[256,128]{1,0:T(8,128)S(1)} %fusion.11, bf16[256,16384]{1,0:T(8,128)(2,1)} %bitcast.78), kind=kOutput, calls=%fused_computation.5 | convolution fusion | flops 6444548096 | bytes 25296896 | tf_op jit(solution)/shard_map/dot_general | solution.py:22
  292.8 0.0 copy-start.1
  292.8 3.4 copy-done.1
  296.2 11.4 %convolution_bitcast_fusion.5 = f32[256,128]{0,1:T(8,128)} fusion(f32[16384,128]{0,1:T(8,128)S(1)} %fusion.2, bf16[256,16384]{1,0:T(8,128)(2,1)} %bitcast.75), kind=kOutput, calls=%fused_computation.9 | convolution fusion | flops 6442450944 | bytes 16908288 | tf_op jit(solution)/shard_map/dot_general | solution.py:15
  307.6 0.0 all-reduce.9.cloned.1.call-update
  307.6 0.3 all-reduce.11.cloned.1.call-start
  307.9 21.4 %all-reduce.9.cloned.1.call-done = f32[256,128]{0,1:T(8,128)} async-done(((f32[256,128]{0,1:T(8,128)}), f32[256,128]{0,1:T(8,128)}) %all-reduce.9.cloned.1.call-update) | async-done | bytes 131088 | tf_op jit(solution)/shard_map/psum | solution.py:18
  329.3 1.3 fusion.8
  330.6 9.4 %fusion.1 = f32[16384,128]{0,1:T(8,128)S(1)} fusion(f32[16384,128]{0,1:T(8,128)} %copy-done.1, f32[256,128]{1,0:T(8,128)S(1)} %fusion.8, bf16[256,16384]{1,0:T(8,128)(2,1)} %bitcast.76), kind=kOutput, calls=%fused_computation.3 | convolution fusion | flops 6444548096 | bytes 25296896 | tf_op jit(solution)/shard_map/dot_general | solution.py:22
  339.9 0.0 copy-start.2
  340.0 3.4 copy-done.2
  343.3 11.4 %convolution_bitcast_fusion.4 = f32[256,128]{0,1:T(8,128)} fusion(f32[16384,128]{0,1:T(8,128)S(1)} %fusion.1, bf16[256,16384]{1,0:T(8,128)(2,1)} %bitcast.73), kind=kOutput, calls=%fused_computation.8 | convolution fusion | flops 6442450944 | bytes 16908288 | tf_op jit(solution)/shard_map/dot_general | solution.py:15
  354.7 0.0 all-reduce.11.cloned.1.call-update
  354.7 21.7 %all-reduce.11.cloned.1.call-done = f32[256,128]{0,1:T(8,128)} async-done(((f32[256,128]{0,1:T(8,128)}), f32[256,128]{0,1:T(8,128)}) %all-reduce.11.cloned.1.call-update) | async-done | bytes 131088 | tf_op jit(solution)/shard_map/psum | solution.py:18
  376.4 1.3 fusion.5
  377.7 12.6 %fusion = f32[16384,128]{0,1:T(8,128)} fusion(f32[16384,128]{0,1:T(8,128)} %copy-done.2, f32[256,128]{1,0:T(8,128)S(1)} %fusion.5, bf16[256,16384]{1,0:T(8,128)(2,1)} %bitcast.74), kind=kOutput, calls=%fused_computation.1 | convolution fusion | flops 6444548096 | bytes 25296896 | tf_op jit(solution)/shard_map/dot_general | solution.py:22
  390.3 9.0 %copy.8 = f32[16384,128]{1,0:T(8,128)} copy(f32[16384,128]{0,1:T(8,128)} %fusion) | data formatting | bytes 16777216 | tf_op jit(solution)/shard_map/sub | solution.py:22
  (1 shorter events, 0.0 us)
Async XLA Ops:
  6.5 173.2 %all-gather.3.cloned.1.call-start = ((), (), s32[]{:S(2)}) async-start(), calls=%async_computation.4 | async-start | bytes 35651584 | tf_op jit(solution)/shard_map/all_gather | solution.py:9
  7.3 227.7 %all-reduce.5.cloned.1.call-start = ((), (), s32[]{:S(2)}) async-start(), calls=%async_computation | async-start | bytes 262144 | tf_op jit(solution)/shard_map/psum | solution.py:18
  200.0 3.2 copy-start.3
  203.2 10.2 %copy-start.4 = (f32[4,256]{1,0:T(4,128)S(1)}, f32[4,256]{1,0:T(4,128)}, u32[]{:S(2)}) copy-start(f32[4,256]{1,0:T(4,128)} %param.6) | copy-start | bytes 12292
  203.2 31.8 %copy-start.5 = (f32[4,256,256]{2,1,0:T(8,128)S(1)}, f32[4,256,256]{2,1,0:T(8,128)}, u32[]{:S(2)}) copy-start(f32[4,256,256]{2,1,0:T(8,128)} %param.7) | copy-start | bytes 3145732
  213.3 68.8 %all-reduce.7.cloned.1.call-start = ((), (), s32[]{:S(2)}) async-start(), calls=%async_computation.1 | async-start | bytes 262144 | tf_op jit(solution)/shard_map/psum | solution.py:18
  245.7 3.4 copy-start
  260.5 68.8 %all-reduce.9.cloned.1.call-start = ((), (), s32[]{:S(2)}) async-start(), calls=%async_computation.2 | async-start | bytes 262144 | tf_op jit(solution)/shard_map/psum | solution.py:18
  292.8 3.4 copy-start.1
  307.6 68.8 %all-reduce.11.cloned.1.call-start = ((), (), s32[]{:S(2)}) async-start(), calls=%async_computation.3 | async-start | bytes 262144 | tf_op jit(solution)/shard_map/psum | solution.py:18
  339.9 3.4 copy-start.2
Sparse Core Ops, SparseCore 0:
  8.9 170.7 all-gather.2
  213.4 21.5 all-reduce.4
  260.6 21.5 all-reduce.6
  307.7 21.5 all-reduce.8
  354.8 21.5 all-reduce.10
